TPU v7x, 8 devices: a whole 2x2x1 slice. The times are simulated.
8 devices in a mesh: dp: 1 (over z), ep: 8 (over y, x, core).
Axes of the slice: x: 2, y: 2, z: 1, core: 2. Of those that a mesh axis runs over, the one named last changes fastest.
Arguments:
- x_tokens: bfloat16 [12288, 2048], P(('dp', 'ep'))
- dy_tokens: bfloat16 [12288, 2048], P(('dp', 'ep'))
- expert_ids: int32 [12288, 6], P(('dp', 'ep'))
- gate_vals: float32 [12288, 6], P(('dp', 'ep'))
- slot_pos: int32 [12288, 6], P(('dp', 'ep'))
- w_gate: bfloat16 [16, 2048, 1408], P('ep')
- w_up: bfloat16 [16, 2048, 1408], P('ep')
- w_down: bfloat16 [16, 1408, 2048], P('ep')
- shared_gate: bfloat16 [2048, 2816], replicated
- shared_up: bfloat16 [2048, 2816], replicated
- shared_down: bfloat16 [2816, 2048], replicated
Outputs:
- output 1: bfloat16 [12288, 2048], P(('dp', 'ep'))
- output 2: float32 [16, 2048, 1408], P(('dp', 'ep'))
- output 3: float32 [16, 2048, 1408], P(('dp', 'ep'))
- output 4: float32 [16, 1408, 2048], P(('dp', 'ep'))
- output 5: float32 [8, 2048, 2816], P(('dp', 'ep'))
- output 6: float32 [8, 2048, 2816], P(('dp', 'ep'))
- output 7: float32 [8, 2816, 2048], P(('dp', 'ep'))
All inputs are finite; a program needn't handle non-finite values.
Results may differ from a plain program's by a relative error of at most 0.00174.
Values are sent between devices in bfloat16 or wider.
A program may use at most 1 GiB of HBM per device.

v0:
```python
import jax
import jax.numpy as jnp
from jax import lax
from jax.sharding import PartitionSpec as P


def swiglu_parts(act_gate, act_up, grad_hidden):
    gate_f32 = act_gate.astype(jnp.float32)
    up_f32 = act_up.astype(jnp.float32)
    sigma = jax.nn.sigmoid(gate_f32)
    silu_gate = gate_f32 * sigma
    hidden = (silu_gate * up_f32).astype(jnp.bfloat16)
    grad_gate = (grad_hidden * up_f32 * sigma * (1.0 + gate_f32 * (1.0 - sigma))).astype(jnp.bfloat16)
    grad_up = (grad_hidden * silu_gate).astype(jnp.bfloat16)
    return hidden, grad_gate, grad_up


def slot_tables(expert_ids, slot_pos, gate_vals, num_experts, capacity):
    tok_count, top_k = expert_ids.shape
    slot_total = num_experts * capacity
    copy_slot = jnp.where(slot_pos >= 0, expert_ids * capacity + slot_pos, slot_total).reshape(-1)
    copy_token = jnp.broadcast_to(jnp.arange(tok_count, dtype=jnp.int32)[:, None], (tok_count, top_k)).reshape(-1)
    slot_token = jnp.full((slot_total + 1,), tok_count, jnp.int32).at[copy_slot].set(copy_token)[:slot_total]
    slot_gate = jnp.zeros((slot_total + 1,), jnp.float32).at[copy_slot].set(gate_vals.reshape(-1))[:slot_total]
    return copy_slot, slot_token, slot_gate


def take_rows(rows, row_index):
    return jnp.take(rows, row_index, axis=0, mode='fill', fill_value=0)


def shared_backward(x_tokens, dy_tokens, shared_gate, shared_up, shared_down):
    act_gate = jnp.dot(x_tokens, shared_gate, preferred_element_type=jnp.float32).astype(jnp.bfloat16)
    act_up = jnp.dot(x_tokens, shared_up, preferred_element_type=jnp.float32).astype(jnp.bfloat16)
    grad_hidden = jnp.einsum('td,fd->tf', dy_tokens, shared_down, preferred_element_type=jnp.float32)
    hidden, grad_gate, grad_up = swiglu_parts(act_gate, act_up, grad_hidden)
    grad_gate_w = jnp.einsum('td,tf->df', x_tokens, grad_gate, preferred_element_type=jnp.float32)
    grad_up_w = jnp.einsum('td,tf->df', x_tokens, grad_up, preferred_element_type=jnp.float32)
    grad_down_w = jnp.einsum('tf,td->fd', hidden, dy_tokens, preferred_element_type=jnp.float32)
    grad_input = jnp.einsum('tf,df->td', grad_gate, shared_gate, preferred_element_type=jnp.float32) + jnp.einsum('tf,df->td', grad_up, shared_up, preferred_element_type=jnp.float32)
    return grad_input, grad_gate_w, grad_up_w, grad_down_w


def solution(mesh):
    group = mesh.shape['ep']
    token_spec = P(('dp', 'ep'), None)
    expert_spec = P('ep', None, None)
    whole_spec = P(None, None)
    grad_spec = P(('dp', 'ep'), None, None)

    def local_backward(x_tokens, dy_tokens, expert_ids, gate_vals, slot_pos, w_gate, w_up, w_down, shared_gate, shared_up, shared_down):
        tok_count, top_k = expert_ids.shape
        local_experts, model_dim, expert_ff = w_gate.shape
        num_experts = local_experts * group
        capacity = (3 * tok_count * top_k + 2 * num_experts - 1) // (2 * num_experts)
        copy_slot, slot_token, slot_gate = slot_tables(expert_ids, slot_pos, gate_vals, num_experts, capacity)
        send_x = take_rows(x_tokens, slot_token).reshape(num_experts, capacity, model_dim)
        dy_rows = take_rows(dy_tokens, slot_token)
        send_dz = (dy_rows.astype(jnp.float32) * slot_gate[:, None]).astype(jnp.bfloat16).reshape(num_experts, capacity, model_dim)
        x_exp = lax.all_to_all(send_x, 'ep', 0, 1, tiled=True)
        dz_exp = lax.all_to_all(send_dz, 'ep', 0, 1, tiled=True)
        act_gate = jnp.einsum('erd,edf->erf', x_exp, w_gate, preferred_element_type=jnp.float32).astype(jnp.bfloat16)
        act_up = jnp.einsum('erd,edf->erf', x_exp, w_up, preferred_element_type=jnp.float32).astype(jnp.bfloat16)
        grad_hidden = jnp.einsum('erd,efd->erf', dz_exp, w_down, preferred_element_type=jnp.float32)
        hidden, grad_gate, grad_up = swiglu_parts(act_gate, act_up, grad_hidden)
        grad_w_gate = jnp.einsum('erd,erf->edf', x_exp, grad_gate, preferred_element_type=jnp.float32)
        grad_w_up = jnp.einsum('erd,erf->edf', x_exp, grad_up, preferred_element_type=jnp.float32)
        grad_w_down = jnp.einsum('erf,erd->efd', hidden, dz_exp, preferred_element_type=jnp.float32)
        grad_exp = (jnp.einsum('erf,edf->erd', grad_gate, w_gate, preferred_element_type=jnp.float32) + jnp.einsum('erf,edf->erd', grad_up, w_up, preferred_element_type=jnp.float32)).astype(jnp.bfloat16)
        returned = lax.all_to_all(grad_exp, 'ep', 1, 0, tiled=True).reshape(num_experts * capacity, model_dim)
        copies = take_rows(returned, copy_slot).reshape(tok_count, top_k, model_dim)
        routed_sum = jnp.sum(copies.astype(jnp.float32), axis=1)
        shared_dx, grad_shared_gate, grad_shared_up, grad_shared_down = shared_backward(x_tokens, dy_tokens, shared_gate, shared_up, shared_down)
        grad_x = (routed_sum + shared_dx).astype(jnp.bfloat16)
        return grad_x, grad_w_gate, grad_w_up, grad_w_down, grad_shared_gate[None], grad_shared_up[None], grad_shared_down[None]

    return jax.shard_map(local_backward, mesh=mesh, in_specs=(token_spec, token_spec, token_spec, token_spec, token_spec, expert_spec, expert_spec, expert_spec, whole_spec, whole_spec, whole_spec), out_specs=(token_spec, grad_spec, grad_spec, grad_spec, grad_spec, grad_spec, grad_spec), check_vma=False)
```

profile of v0, /device:TPU:0, one launch (start us, length us, event | category | flops | bytes accessed | tf_op | source)
XLA Modules:
  0.0 2888.9 jit_solution(16164717918254490822)
XLA Ops:
  4.2 34.2 %scatter_custom_fusion = s32[13825]{0:T(1024)S(1)} fusion(s32[9216]{0:T(1024)S(1)} %bitcast.71, s32[9216]{0:T(1024)S(1)} %reshape.135, s32[]{:T(128)} %constant.14.clone.1), kind=kCustom, calls=%fused_computation.56 | custom fusion | bytes 55304 | tf_op jit(solution)/shard_map/scatter | solution.py:23
  38.5 105.8 %gather_fusion.2 = bf16[13824,2048]{1,0:T(8,128)(2,1)} fusion(bf16[1536,2048]{1,0:T(8,128)(2,1)} %param.13, s32[14336]{0:T(1024)S(1)} %pad_clamp_fusion), kind=kCustom, calls=%fused_computation.1.clone | custom fusion | bytes 113301504 | tf_op jit(solution)/shard_map/jit(_take)/gather | solution.py:29
  144.3 37.5 %broadcast_select_fusion = bf16[13824,2048]{1,0:T(8,128)(2,1)} fusion(bf16[13824,2048]{1,0:T(8,128)(2,1)} %gather_fusion.2, pred[13824]{0:T(1024)(128)(4,1)S(1)} %compare_and_fusion), kind=kLoop, calls=%fused_computation.22 | loop fusion | flops 28311552 | bytes 113260032 | tf_op jit(solution)/shard_map/jit(_take)/select_n | solution.py:29
  190.7 105.9 %gather_fusion.1 = bf16[13824,2048]{1,0:T(8,128)(2,1)} fusion(bf16[1536,2048]{1,0:T(8,128)(2,1)} %param.14, s32[14336]{0:T(1024)S(1)} %pad_clamp_fusion), kind=kCustom, calls=%fused_computation.clone | custom fusion | bytes 113301504 | tf_op jit(solution)/shard_map/jit(_take)/gather | solution.py:29
  296.5 34.4 %scatter_custom_fusion.1 = f32[13825]{0:T(1024)S(1)} fusion(s32[9216]{0:T(1024)} %bitcast.72, f32[9216]{0:T(1024)S(1)} %reshape.143, f32[]{:T(128)} %constant.23.clone.1), kind=kCustom, calls=%fused_computation.54 | custom fusion | bytes 55812 | tf_op jit(solution)/shard_map/scatter | solution.py:24
  330.9 37.9 %multiply_convert_fusion = bf16[13824,2048]{1,0:T(8,128)(2,1)} fusion(bf16[13824,2048]{1,0:T(8,128)(2,1)} %gather_fusion.1, f32[13824]{0:T(1024)S(1)} %bitcast.69, pred[13824]{0:T(1024)(128)(4,1)S(1)} %copy-done.4), kind=kLoop, calls=%fused_computation.9 | loop fusion | flops 113246208 | bytes 113315328 | tf_op jit(solution)/shard_map/convert_element_type | solution.py:59
  368.9 433.2 %all-to-all-done.1 = bf16[16,864,2048]{2,1,0:T(8,128)(2,1)} async-done(((bf16[16,864,2048]{2,1,0:T(8,128)(2,1)}), bf16[16,864,2048]{2,1,0:T(8,128)(2,1)}, u32[]{:S(2)}, u32[]{:S(2)}) %all-to-all-start.1) | async-done | bytes 56623136 | tf_op jit(solution)/shard_map/all_to_all | solution.py:60
  810.2 24.8 convolution_convert_fusion.2
  835.0 23.4 convolution_convert_fusion.3
  858.4 32.6 %fusion.12 = (bf16[1536,2816]{1,0:T(8,128)(2,1)}, f32[1536,2816]{1,0:T(8,128)}) fusion(bf16[1536,2816]{1,0:T(8,128)(2,1)} %convolution_convert_fusion.3, bf16[1536,2816]{1,0:T(8,128)(2,1)} %convolution_convert_fusion.2, bf16[1536,2048]{1,0:T(8,128)(2,1)} %param.14, bf16[2816,2048]{1,0:T(8,128)(2,1)} %param.23), kind=kOutput, calls=%fused_computation.33 | convolution fusion | flops 17768644608 | bytes 61079552 | tf_op jit(solution)/shard_map/td,fd->tf/dot_general | solution.py:35
  891.0 24.8 fusion.26
  915.8 30.6 %convolution_bitcast_fusion.1 = f32[1,2048,2816]{1,2,0:T(8,128)} fusion(bf16[1536,2048]{1,0:T(8,128)(2,1)} %param.13, f32[1536,2816]{1,0:T(8,128)} %get-tuple-element.36, bf16[1536,2816]{1,0:T(8,128)(2,1)} %convolution_convert_fusion.2), kind=kOutput, calls=%fused_computation.41 | convolution fusion | flops 17747017728 | bytes 55312384 | tf_op jit(solution)/shard_map/td,tf->df/dot_general | solution.py:38
  946.4 37.4 %copy.40 = bf16[2,8,864,2048]{3,2,1,0:T(8,128)(2,1)} copy(bf16[2,8,864,2048]{3,2,0,1:T(8,128)(2,1)} %bitcast.7) | data formatting | bytes 113246208 | tf_op jit(solution)/shard_map/all_to_all | solution.py:60
  983.8 96.7 %convolution_convert_fusion = bf16[2,6912,1408]{2,1,0:T(8,128)(2,1)} fusion(bf16[2,6912,2048]{2,1,0:T(8,128)(2,1)} %bitcast.63, bf16[2,2048,1408]{2,1,0:T(8,128)(2,1)} %param.18), kind=kOutput, calls=%fused_computation.24 | convolution fusion | flops 79744794624 | bytes 107085824 | tf_op jit(solution)/shard_map/erd,edf->erf/dot_general | solution.py:62
  1080.5 96.8 %convolution_convert_fusion.1 = bf16[2,6912,1408]{2,1,0:T(8,128)(2,1)} fusion(bf16[2,6912,2048]{2,1,0:T(8,128)(2,1)} %bitcast.64, bf16[2,2048,1408]{2,1,0:T(8,128)(2,1)} %param.19), kind=kOutput, calls=%fused_computation.25 | convolution fusion | flops 79744794624 | bytes 107085824 | tf_op jit(solution)/shard_map/erd,edf->erf/dot_general | solution.py:63
  1177.3 244.3 %all-to-all-done = bf16[16,864,2048]{2,1,0:T(8,128)(2,1)} async-done(((bf16[16,864,2048]{2,1,0:T(8,128)(2,1)}), bf16[16,864,2048]{2,1,0:T(8,128)(2,1)}, u32[]{:S(2)}, u32[]{:S(2)}) %all-to-all-start) | async-done | bytes 56623136 | tf_op jit(solution)/shard_map/all_to_all | solution.py:61
  1421.5 37.4 %copy.39 = bf16[2,8,864,2048]{3,2,1,0:T(8,128)(2,1)} copy(bf16[2,8,864,2048]{3,2,0,1:T(8,128)(2,1)} %bitcast.3) | data formatting | bytes 113246208 | tf_op jit(solution)/shard_map/all_to_all | solution.py:61
  1458.9 123.2 %multiply_convert_fusion.1 = (bf16[2,6912,1408]{2,1,0:T(8,128)(2,1)}, bf16[2,6912,1408]{2,1,0:T(8,128)(2,1)}) fusion(bf16[2,6912,1408]{2,1,0:T(8,128)(2,1)} %convolution_convert_fusion, bf16[2,6912,1408]{2,1,0:T(8,128)(2,1)} %convolution_convert_fusion.1, bf16[2,6912,2048]{2,1,0:T(8,128)(2,1)} %bitcast.67, bf16[2,1408,2048]{2,1,0:T(8,128)(2,1)} %param.20), kind=kOutput, calls=%fused_computation.21 | convolution fusion | flops 80017293312 | bytes 223870976 | tf_op jit(solution)/shard_map/erd,efd->erf/dot_general | solution.py:64
  1582.1 99.1 %fusion.25 = f32[2,6912,2048]{2,1,0:T(8,128)} fusion(bf16[2,6912,1408]{2,1,0:T(8,128)(2,1)} %get-tuple-element.32, bf16[2,2048,1408]{2,1,0:T(8,128)(2,1)} %param.18), kind=kOutput, calls=%fused_computation.61 | convolution fusion | flops 79725330432 | bytes 163708928 | tf_op jit(solution)/shard_map/erf,edf->erd/dot_general | solution.py:69
  1681.2 100.0 %add_convert_fusion = bf16[2,6912,2048]{2,1,0:T(8,128)(2,1)} fusion(f32[2,6912,2048]{2,1,0:T(8,128)} %fusion.25, bf16[2,6912,1408]{2,1,0:T(8,128)(2,1)} %get-tuple-element.31, bf16[2,2048,1408]{2,1,0:T(8,128)(2,1)} %param.19), kind=kOutput, calls=%fused_computation.8 | convolution fusion | flops 79781953536 | bytes 220332032 | tf_op jit(solution)/shard_map/erf,edf->erd/dot_general | solution.py:69
  1781.2 100.1 %copy.41 = bf16[2,6912,2048]{2,0,1:T(2,128)(2,1)} copy(bf16[2,6912,2048]{2,1,0:T(8,128)(2,1)} %add_convert_fusion) | data formatting | bytes 113246208 | tf_op jit(solution)/shard_map/convert_element_type | solution.py:69
  1889.2 25.4 convolution_bitcast_fusion.2
  1962.7 30.7 %convolution_bitcast_fusion = f32[1,2816,2048]{2,1,0:T(8,128)} fusion(bf16[1536,2048]{1,0:T(8,128)(2,1)} %param.14, bf16[1536,2816]{1,0:T(8,128)(2,1)} %convolution_convert_fusion.3, bf16[1536,2816]{1,0:T(8,128)(2,1)} %convolution_convert_fusion.2), kind=kOutput, calls=%fused_computation.40 | convolution fusion | flops 17751343104 | bytes 46661632 | tf_op jit(solution)/shard_map/tf,td->fd/dot_general | solution.py:39
  1993.4 98.0 %fusion.28 = f32[2,2048,1408]{2,1,0:T(8,128)} fusion(bf16[2,6912,2048]{2,1,0:T(8,128)(2,1)} %bitcast.65, bf16[2,6912,1408]{2,1,0:T(8,128)(2,1)} %get-tuple-element.31), kind=kOutput, calls=%fused_computation.64 | convolution fusion | flops 79725330432 | bytes 118620160 | tf_op jit(solution)/shard_map/erd,erf->edf/dot_general | solution.py:67
  2091.4 98.1 %fusion.27 = f32[2,2048,1408]{2,1,0:T(8,128)} fusion(bf16[2,6912,2048]{2,1,0:T(8,128)(2,1)} %bitcast.66, bf16[2,6912,1408]{2,1,0:T(8,128)(2,1)} %get-tuple-element.32), kind=kOutput, calls=%fused_computation.63 | convolution fusion | flops 79725330432 | bytes 118620160 | tf_op jit(solution)/shard_map/erd,erf->edf/dot_general | solution.py:66
  2189.5 106.7 %fusion.8 = f32[2,1408,2048]{2,1,0:T(8,128)} fusion(bf16[2,6912,2048]{2,1,0:T(8,128)(2,1)} %bitcast.68, bf16[2,6912,1408]{2,1,0:T(8,128)(2,1)} %convolution_convert_fusion.1, bf16[2,6912,1408]{2,1,0:T(8,128)(2,1)} %convolution_convert_fusion), kind=kOutput, calls=%fused_computation.23 | convolution fusion | flops 79881043968 | bytes 157548544 | tf_op jit(solution)/shard_map/erf,erd->efd/dot_general | solution.py:68
  2296.2 204.3 %all-to-all-done.2 = bf16[2,6912,2048]{2,0,1:T(2,128)(2,1)} async-done(((bf16[2,6912,2048]{2,0,1:T(2,128)(2,1)}), bf16[2,6912,2048]{2,0,1:T(2,128)(2,1)}, u32[]{:S(2)}, u32[]{:S(2)}) %all-to-all-start.2) | async-done | bytes 56623136 | tf_op jit(solution)/shard_map/all_to_all | solution.py:70
  2500.5 37.5 %copy.42 = bf16[2,8,864,2048]{3,2,0,1:T(8,128)(2,1)} copy(bf16[2,8,864,2048]{3,0,2,1:T(2,128)(2,1)} %bitcast.9) | data formatting | bytes 113246208 | tf_op jit(solution)/shard_map/all_to_all | solution.py:70
  2538.0 216.2 %gather_fusion = bf16[9216,2048]{1,0:T(8,128)(2,1)} fusion(bf16[13824,2048]{1,0:T(8,128)(2,1)} %bitcast.60, s32[9216]{0:T(1024)S(1)} %copy-done.1), kind=kCustom, calls=%fused_computation.2 | custom fusion | bytes 75534336 | tf_op jit(solution)/shard_map/jit(_take)/gather | solution.py:29
  2754.2 58.6 %gather.10 = bf16[1536,6,2048]{2,1,0:T(8,128)(2,1)} reshape(bf16[9216,2048]{1,0:T(8,128)(2,1)} %gather_fusion) | data formatting | bytes 75497472 | tf_op jit(solution)/shard_map/jit(_take)/gather | solution.py:29
  2812.7 46.7 %convert_reduce_fusion = f32[1536,2048]{1,0:T(8,128)} fusion(bf16[1536,6,2048]{2,1,0:T(8,128)(2,1)} %gather.10, pred[1536,6]{1,0:T(8,128)(4,1)S(1)} %copy-done), kind=kLoop, calls=%fused_computation.10 | loop fusion | flops 53477376 | bytes 50340864 | tf_op jit(solution)/shard_map/reduce_sum | solution.py:72
  2859.4 29.0 %add_convert_fusion.1 = bf16[1536,2048]{1,0:T(8,128)(2,1)} fusion(f32[1536,2048]{1,0:T(8,128)} %convert_reduce_fusion, f32[1536,2048]{1,0:T(8,128)} %fusion.26, bf16[2048,2816]{1,0:T(8,128)(2,1)} %param.22, f32[1536,2816]{1,0:T(8,128)} %get-tuple-element.36, bf16[1536,2816]{1,0:T(8,128)(2,1)} %convolution_convert_fusion.2), kind=kOutput, calls=%fused_computation.43 | convolution fusion | flops 17756454912 | bytes 68943872 | tf_op jit(solution)/shard_map/tf,df->td/dot_general | solution.py:40
  (39 shorter events, 76.5 us)
Async XLA Ops:
  3.6 34.9 %copy-start.7 = (s32[9216,1]{0,1:T(1,128)}, s32[9216,1]{0,1:T(1,128)S(1)}, u32[]{:S(2)}) copy-start(s32[9216,1]{0,1:T(1,128)S(1)} %get-tuple-element.34) | copy-start | bytes 110596
  38.5 105.8 %copy-start.3 = (pred[13824]{0:T(1024)(128)(4,1)}, pred[13824]{0:T(1024)(128)(4,1)S(1)}, u32[]{:S(2)}) copy-start(pred[13824]{0:T(1024)(128)(4,1)S(1)} %compare_and_fusion) | copy-start | bytes 41476
  181.9 7.9 copy-start.5
  181.9 620.2 %all-to-all-start.1 = ((bf16[16,864,2048]{2,1,0:T(8,128)(2,1)}), bf16[16,864,2048]{2,1,0:T(8,128)(2,1)}, u32[]{:S(2)}, u32[]{:S(2)}) async-start(bf16[16,864,2048]{2,1,0:T(8,128)(2,1)} %bitcast.61), calls=%async_computation.1 | async-start | bytes 113246208 | tf_op jit(solution)/shard_map/all_to_all | solution.py:60
  190.6 140.3 %copy-start.4 = (pred[13824]{0:T(1024)(128)(4,1)S(1)}, pred[13824]{0:T(1024)(128)(4,1)}, u32[]{:S(2)}) copy-start(pred[13824]{0:T(1024)(128)(4,1)} %copy-done.3) | copy-start | bytes 41476
  802.1 32.9 %slice-start = ((s8[6291456]{0:T(1024)(128)(4,1)}), s8[2097152]{0:T(1024)(128)(4,1)S(1)}, s32[]{:S(2)}) async-start(s8[6291456]{0:T(1024)(128)(4,1)} %bitcast.58), calls=%async_computation.3 | async-start | bytes 4194304
  802.1 619.4 %all-to-all-start = ((bf16[16,864,2048]{2,1,0:T(8,128)(2,1)}), bf16[16,864,2048]{2,1,0:T(8,128)(2,1)}, u32[]{:S(2)}, u32[]{:S(2)}) async-start(bf16[16,864,2048]{2,1,0:T(8,128)(2,1)} %bitcast.62), calls=%async_computation | async-start | bytes 113246208 | tf_op jit(solution)/shard_map/all_to_all | solution.py:61
  810.2 24.8 slice-start.1
  1881.4 619.1 %all-to-all-start.2 = ((bf16[2,6912,2048]{2,0,1:T(2,128)(2,1)}), bf16[2,6912,2048]{2,0,1:T(2,128)(2,1)}, u32[]{:S(2)}, u32[]{:S(2)}) async-start(bf16[2,6912,2048]{2,0,1:T(2,128)(2,1)} %copy.41), calls=%async_computation.2 | async-start | bytes 113246208 | tf_op jit(solution)/shard_map/all_to_all | solution.py:70
  1889.2 25.4 copy-start.6
  1938.8 23.3 copy-start.2
  2500.5 37.5 %copy-start.1 = (s32[9216]{0:T(1024)S(1)}, s32[9216]{0:T(1024)}, u32[]{:S(2)}) copy-start(s32[9216]{0:T(1024)} %broadcast_clamp_fusion) | copy-start | bytes 110596
  2754.2 58.6 %copy-start = (pred[1536,6]{1,0:T(8,128)(4,1)S(1)}, pred[1536,6]{1,0:T(8,128)(4,1)}, u32[]{:S(2)}) copy-start(pred[1536,6]{1,0:T(8,128)(4,1)} %copy.36) | copy-start | bytes 27652
where the time goes:
time: 2900 us; the launch traced here: 2890 us
  matrix products  1040 us (36%)
  waiting for transfers between devices  882 us (30%)
  local copies, waits for them, and re-layouts  817 us (28%)
  other arithmetic  125 us (4%)
    gather x4, local copies, waits for them, and re-layouts, take_rows(): return jnp.take(rows, row_index, axis=0, mode='fill', fill_value=0)  486 us
    all_to_all x1, waiting for transfers between devices, local_backward(): x_exp = lax.all_to_all(send_x, 'ep', 0, 1, tiled=True)  433 us
    all_to_all x1, waiting for transfers between devices, local_backward(): dz_exp = lax.all_to_all(send_dz, 'ep', 0, 1, tiled=True)  244 us
    all_to_all x1, waiting for transfers between devices, local_backward(): lax.all_to_all(grad_exp, 'ep', 1, 0, tiled=True)  204 us
    dot_general x1, matrix products, local_backward(): jnp.einsum('erd,efd->erf', dz_exp, w_down, preferred_element_type=jnp.flo...  123 us
    dot_general x1, matrix products, local_backward(): jnp.einsum('erf,erd->efd', hidden, dz_exp, preferred_element_type=jnp.flo...  107 us
    convert_element_type x1, local copies, waits for them, and re-layouts, local_backward(): (jnp.einsum('erf,edf->erd', grad_gate, w_gate, preferred_element_type=jnp...  100 us
    dot_general x1, matrix products, local_backward(): jnp.einsum('erf,edf->erd', grad_up, w_up, preferred_element_type=jnp.floa...  100 us
  transfers between devices with their start and end apart: 3, of which 3 were waited for; matrix products, arithmetic and copies ran while one was open for 33% of the time, Pallas kernels for 0%

commit v1 on v0

v1 whole, which is shorter than its diff:
```python
import functools

import jax
import jax.numpy as jnp
from jax import lax
from jax.experimental import pallas as pl
from jax.experimental.pallas import tpu as pltpu
from jax.sharding import PartitionSpec as P

BF16, F32, I32 = jnp.bfloat16, jnp.float32, jnp.int32
TB = 256
TM = 512
CHUNKS = 2
VMEM = 64 * 1024 * 1024 - 128 * 1024


def dot(a, b):
    return lax.dot_general(a, b, (((1,), (0,)), ((), ())), preferred_element_type=F32)


def dot_t(a, b):
    return lax.dot_general(a, b, (((1,), (1,)), ((), ())), preferred_element_type=F32)


def params(ndim):
    return pltpu.CompilerParams(dimension_semantics=("arbitrary",) * ndim, vmem_limit_bytes=VMEM)


def swiglu_parts(act_gate, act_up, grad_hidden):
    gate_f32 = act_gate.astype(F32)
    up_f32 = act_up.astype(F32)
    sigma = jax.nn.sigmoid(gate_f32)
    silu_gate = gate_f32 * sigma
    hidden = (silu_gate * up_f32).astype(BF16)
    grad_gate = (grad_hidden * up_f32 * sigma * (1.0 + gate_f32 * (1.0 - sigma))).astype(BF16)
    grad_up = (grad_hidden * silu_gate).astype(BF16)
    return hidden, grad_gate, grad_up


def pack_kernel(tile_ref, x_ref, dy_ref, pos_ref, gate_ref, *refs):
    xo_ref, zo_ref = refs[-2:]
    e, b, k = pl.program_id(0), pl.program_id(1), pl.program_id(2)
    blocks = pl.num_programs(1) - 1
    step = 2 * b + k
    tile = tile_ref[e, step]
    before = tile_ref[e, jnp.maximum(step - 1, 0)]
    fresh = (step == 0) | (tile != before)

    @pl.when(fresh)
    def _():
        xo_ref[...] = jnp.zeros_like(xo_ref)
        zo_ref[...] = jnp.zeros_like(zo_ref)

    @pl.when((b < blocks) & ((k == 0) | fresh))
    def _():
        local = pos_ref[0, 0] - tile * TB
        hit = lax.broadcasted_iota(I32, (TB, TB), 0) == local
        row_gate = jnp.sum(jnp.where(hit, gate_ref[0, 0], 0.0), axis=1, keepdims=True)
        pick = hit.astype(F32).astype(BF16)
        xo_ref[0] += dot(pick, x_ref[...]).astype(BF16)
        zo_ref[0] += (dot(pick, dy_ref[...]) * row_gate).astype(BF16)


def pack_rows(tiles, x, dy, pos, gate, after):
    experts, blocks = pos.shape[:2]
    rows, dim = x.shape
    tok = lambda e, b, k, t: (jnp.minimum(b, blocks - 1), 0)
    row = lambda e, b, k, t: (e, jnp.minimum(b, blocks - 1), 0, 0)
    out = lambda e, b, k, t: (e, t[e, 2 * b + k], 0)
    return pl.pallas_call(
        pack_kernel,
        grid_spec=pltpu.PrefetchScalarGridSpec(
            num_scalar_prefetch=1, grid=(experts, blocks + 1, 2),
            in_specs=[pl.BlockSpec((TB, dim), tok), pl.BlockSpec((TB, dim), tok),
                      pl.BlockSpec((1, 1, 1, TB), row), pl.BlockSpec((1, 1, 1, TB), row)] + [pl.BlockSpec(memory_space=pl.ANY)] * len(after),
            out_specs=[pl.BlockSpec((1, TB, dim), out), pl.BlockSpec((1, TB, dim), out)]),
        out_shape=[jax.ShapeDtypeStruct((experts, rows, dim), BF16)] * 2,
        compiler_params=params(3),
        cost_estimate=pl.CostEstimate(flops=30_000_000_000, bytes_accessed=200_000_000, transcendentals=0),
        name="pack_rows",
    )(tiles, x, dy, pos, gate, *after)


def ffn_kernel(n_ref, x_ref, z_ref, w1_ref, w3_ref, w2_ref, h_ref, d_ref, r_ref):
    ff = w1_ref.shape[2]
    dim = w1_ref.shape[1]

    @pl.when(pl.program_id(1) < n_ref[pl.program_id(0)])
    def _():
        def columns(lo, size, act_gate, act_up):
            grad_hidden = dot_t(z_ref[0], w2_ref[0, lo:lo + size, :])
            hidden, grad_gate, grad_up = swiglu_parts(act_gate.astype(BF16), act_up.astype(BF16), grad_hidden)
            h_ref[0, :, lo:lo + size] = hidden
            d_ref[0, :, lo:lo + size] = grad_gate
            d_ref[0, :, ff + lo:ff + lo + size] = grad_up

        full = ff // 256 * 256
        for lo in range(0, full, 256):
            columns(lo, 256, dot(x_ref[0], w1_ref[0, :, lo:lo + 256]), dot(x_ref[0], w3_ref[0, :, lo:lo + 256]))
        if full < ff:
            both = dot(x_ref[0], jnp.concatenate([w1_ref[0, :, full:], w3_ref[0, :, full:]], axis=1))
            columns(full, ff - full, both[:, :ff - full], both[:, ff - full:])
        for lo in range(0, dim, 256):
            w = jnp.concatenate([w1_ref[0, lo:lo + 256, :], w3_ref[0, lo:lo + 256, :]], axis=1)
            r_ref[0, :, lo:lo + 256] = dot_t(d_ref[0], w).astype(r_ref.dtype)


def ffn_tiles(active, x, z, w1, w3, w2, out_dtype, tm, name):
    experts, rows, dim = x.shape
    ff = w1.shape[2]
    tile = lambda e, m, n: (e, jnp.minimum(m, n[e] - 1), 0)
    whole = lambda e, m, n: (e, 0, 0)
    return pl.pallas_call(
        ffn_kernel,
        grid_spec=pltpu.PrefetchScalarGridSpec(
            num_scalar_prefetch=1, grid=(experts, rows // tm),
            in_specs=[pl.BlockSpec((1, tm, dim), tile), pl.BlockSpec((1, tm, dim), tile),
                      pl.BlockSpec((1, dim, ff), whole, pipeline_mode=pl.Buffered(1)),
                      pl.BlockSpec((1, dim, ff), whole, pipeline_mode=pl.Buffered(1)),
                      pl.BlockSpec((1, ff, dim), whole, pipeline_mode=pl.Buffered(1))],
            out_specs=[pl.BlockSpec((1, tm, ff), tile), pl.BlockSpec((1, tm, 2 * ff), tile),
                       pl.BlockSpec((1, tm, dim), tile)]),
        out_shape=[jax.ShapeDtypeStruct((experts, rows, ff), BF16),
                   jax.ShapeDtypeStruct((experts, rows, 2 * ff), BF16),
                   jax.ShapeDtypeStruct((experts, rows, dim), out_dtype)],
        compiler_params=params(2),
        cost_estimate=pl.CostEstimate(flops=5 * rows * dim * ff, bytes_accessed=150_000_000, transcendentals=0),
        name=name,
    )(active, x, z, w1, w3, w2)


def tile_maps(chunks):
    def maker(c, cols):
        def index(e, d, j, n):
            first = sum((n[q, e] for q in range(c)), 0)
            return (e, jnp.clip(j - first, 0, n[c, e] - 1), d if cols else 0)
        return index
    return [maker(c, False) for c in range(chunks)], [maker(c, True) for c in range(chunks)]


def for_chunk(n_ref, chunks, body):
    e, j = pl.program_id(0), pl.program_id(2)
    first = 0
    for c in range(chunks):
        last = first + n_ref[c, e]
        pl.when((j >= first) & (j < last))(functools.partial(body, c))
        first = last


def up_grad_kernel(chunks, n_ref, *refs):
    xs, ds = refs[:chunks], refs[chunks:2 * chunks]
    g1_ref, g3_ref = refs[2 * chunks:]
    ff = g1_ref.shape[2]

    @pl.when(pl.program_id(2) == 0)
    def _():
        g1_ref[...] = jnp.zeros_like(g1_ref)
        g3_ref[...] = jnp.zeros_like(g3_ref)

    def body(c):
        x_t = xs[c][0].T
        for lo in range(0, 2 * ff, 256):
            part = dot(x_t, ds[c][0, :, lo:lo + 256])
            if lo + 256 <= ff:
                g1_ref[0, :, lo:lo + 256] += part
            elif lo >= ff:
                g3_ref[0, :, lo - ff:lo - ff + 256] += part
            else:
                g1_ref[0, :, lo:] += part[:, :ff - lo]
                g3_ref[0, :, :lo + 256 - ff] += part[:, ff - lo:]

    for_chunk(n_ref, chunks, body)


def up_grads(active, xs, ds, split):
    chunks = len(xs)
    experts, rows, dim = xs[0].shape
    ff = ds[0].shape[2] // 2
    whole, cols = tile_maps(chunks)
    out = lambda e, d, j, n: (e, d, 0)
    return pl.pallas_call(
        functools.partial(up_grad_kernel, chunks),
        grid_spec=pltpu.PrefetchScalarGridSpec(
            num_scalar_prefetch=1, grid=(experts, split, chunks * (rows // TM)),
            in_specs=[pl.BlockSpec((1, TM, dim // split), m) for m in cols] + [pl.BlockSpec((1, TM, 2 * ff), m) for m in whole],
            out_specs=[pl.BlockSpec((1, dim // split, ff), out)] * 2),
        out_shape=[jax.ShapeDtypeStruct((experts, dim, ff), F32)] * 2,
        compiler_params=params(3),
        cost_estimate=pl.CostEstimate(flops=120_000_000_000, bytes_accessed=250_000_000, transcendentals=0),
        name="up_grads",
    )(active, *xs, *ds)


def down_grad_kernel(chunks, n_ref, *refs):
    hs, zs = refs[:chunks], refs[chunks:2 * chunks]
    g_ref = refs[2 * chunks]

    @pl.when(pl.program_id(2) == 0)
    def _():
        g_ref[...] = jnp.zeros_like(g_ref)

    def body(c):
        h_t = hs[c][0].T
        for lo in range(0, g_ref.shape[2], 256):
            g_ref[0, :, lo:lo + 256] += dot(h_t, zs[c][0, :, lo:lo + 256])

    for_chunk(n_ref, chunks, body)


def down_grads(active, hs, zs, split):
    chunks = len(hs)
    experts, rows, ff = hs[0].shape
    dim = zs[0].shape[2]
    whole, cols = tile_maps(chunks)
    return pl.pallas_call(
        functools.partial(down_grad_kernel, chunks),
        grid_spec=pltpu.PrefetchScalarGridSpec(
            num_scalar_prefetch=1, grid=(experts, split, chunks * (rows // TM)),
            in_specs=[pl.BlockSpec((1, TM, ff), m) for m in whole] + [pl.BlockSpec((1, TM, dim // split), m) for m in cols],
            out_specs=[pl.BlockSpec((1, ff, dim // split), lambda e, d, j, n: (e, 0, d))]),
        out_shape=[jax.ShapeDtypeStruct((experts, ff, dim), F32)],
        compiler_params=params(3),
        cost_estimate=pl.CostEstimate(flops=60_000_000_000, bytes_accessed=150_000_000, transcendentals=0),
        name="down_grads",
    )(active, *hs, *zs)[0]


def token_sum_kernel(experts, lo_ref, hi_ref, pos_ref, *refs):
    b = pl.program_id(0)
    out_ref = refs[-1]
    picks, rows = [], []
    for e in range(experts):
        for near, tile_ref in enumerate((lo_ref, hi_ref)):
            tile = tile_ref[e, b]
            local = jnp.where(tile < 0, -1, pos_ref[e, 0] - tile * TB)
            picks.append((lax.broadcasted_iota(I32, (TB, TB), 0) == local).astype(F32).T.astype(BF16))
            rows.append(refs[2 * e + near][0])
    out_ref[...] = dot(jnp.concatenate(picks, axis=1), jnp.concatenate(rows, axis=0))


def token_sums(lo, hi, pos, r):
    experts, blocks = pos.shape[:2]
    dim = r.shape[2]
    specs = []
    for e in range(experts):
        specs.append(pl.BlockSpec((1, TB, dim), lambda b, l, h, e=e: (e, jnp.maximum(l[e, b], 0), 0)))
        specs.append(pl.BlockSpec((1, TB, dim), lambda b, l, h, e=e: (e, jnp.maximum(h[e, b], 0), 0)))
    return pl.pallas_call(
        functools.partial(token_sum_kernel, experts),
        grid_spec=pltpu.PrefetchScalarGridSpec(
            num_scalar_prefetch=2, grid=(blocks,),
            in_specs=[pl.BlockSpec((experts, 1, 1, TB), lambda b, l, h: (0, b, 0, 0))] + specs,
            out_specs=[pl.BlockSpec((TB, dim), lambda b, l, h: (b, 0))]),
        out_shape=[jax.ShapeDtypeStruct((blocks * TB, dim), F32)],
        compiler_params=params(1),
        cost_estimate=pl.CostEstimate(flops=20_000_000_000, bytes_accessed=100_000_000, transcendentals=0),
        name="token_sums",
    )(lo, hi, pos, *([r] * (2 * experts)))[0]


def shared_backward(x, dy, gate_w, up_w, down_w):
    x, dy = x[None], dy[None]
    tm = x.shape[1] // 4
    all_tiles = lambda size: jnp.full((1,), x.shape[1] // size, I32)
    hidden, grads, back = ffn_tiles(all_tiles(tm), x, dy, gate_w[None], up_w[None], down_w[None], F32, tm, "shared_ffn")
    grad_gate, grad_up = up_grads(all_tiles(TM)[None], [x], [grads], 4)
    grad_down = down_grads(all_tiles(TM)[None], [hidden], [dy], 2)
    return back[0], grad_gate, grad_up, grad_down


def chunk_tables(codes, gates, experts):
    top_k, tokens = codes.shape
    blocks = tokens // TB
    ids = lax.axis_index('ep') * experts + jnp.arange(experts, dtype=I32)
    match = codes[None] == ids[:, None, None].astype(F32)
    hit = jnp.any(match, axis=1).reshape(experts, blocks, TB)
    gate = jnp.sum(jnp.where(match, gates[None], 0.0), axis=1).reshape(experts, blocks, 1, TB)
    tri = (jnp.arange(TB)[:, None] < jnp.arange(TB)[None, :]).astype(BF16)
    rank = jnp.dot(hit.reshape(-1, TB).astype(BF16), tri, preferred_element_type=F32).astype(I32).reshape(experts, blocks, TB)
    count = jnp.sum(hit.astype(I32), axis=2)
    below = jnp.arange(blocks)[:, None] < jnp.arange(blocks)[None, :]
    start = jnp.sum(jnp.where(below[None], count[:, :, None], 0), axis=1)
    total = start[:, -1] + count[:, -1]
    pos = jnp.where(hit, start[:, :, None] + rank, -(1 << 20)).reshape(experts, blocks, 1, TB)
    active = jnp.maximum((total + TM - 1) // TM, 1)
    small_last = jnp.maximum((total + TB - 1) // TB, 1)[:, None] - 1
    lo = jnp.minimum(start // TB, small_last)
    hi = jnp.clip((start + count - 1) // TB, lo, small_last)
    visits = jnp.stack([lo, hi], axis=2).reshape(experts, 2 * blocks)
    tail = (active * (TM // TB) - 1)[:, None]
    visits = jnp.concatenate([visits, tail, tail], axis=1)
    some = count > 0
    return visits, active, jnp.where(some, lo, -1), jnp.where(some & (hi > lo), hi, -1), pos, gate


def solution(mesh):
    group = mesh.shape['ep']
    token_spec = P(('dp', 'ep'), None)
    expert_spec = P('ep', None, None)
    whole_spec = P(None, None)
    grad_spec = P(('dp', 'ep'), None, None)

    def local_backward(x_tokens, dy_tokens, expert_ids, gate_vals, slot_pos, w_gate, w_up, w_down, shared_gate, shared_up, shared_down):
        tok_count, top_k = expert_ids.shape
        local_experts = w_gate.shape[0]
        part = tok_count // CHUNKS
        codes = jnp.where(slot_pos >= 0, expert_ids, -1).astype(F32).T
        plan = lax.all_gather(jnp.concatenate([codes, gate_vals.T], axis=0), 'ep', axis=0)
        gathered = []
        for c in range(CHUNKS):
            rows = slice(c * part, (c + 1) * part)
            gathered.append((lax.all_gather(x_tokens[rows], 'ep', axis=0, tiled=True), lax.all_gather(dy_tokens[rows], 'ep', axis=0, tiled=True)))
        shared = shared_backward(x_tokens, dy_tokens, shared_gate, shared_up, shared_down)
        shared_dx, grad_shared_gate, grad_shared_up, grad_shared_down = shared
        packed = []
        for c in range(CHUNKS):
            mine = plan[:, :, c * part:(c + 1) * part].transpose(1, 0, 2).reshape(2 * top_k, group * part)
            visits, active, lo, hi, pos, gate = chunk_tables(mine[:top_k], mine[top_k:], local_experts)
            x_rows, z_rows = pack_rows(visits, *gathered[c], pos, gate, shared[1:] if c == 0 else ())
            hidden, grads, back = ffn_tiles(active, x_rows, z_rows, w_gate, w_up, w_down, BF16, TM, "ffn_tiles")
            summed = lax.psum_scatter(token_sums(lo, hi, pos, back), 'ep', scatter_dimension=0, tiled=True)
            packed.append((active, x_rows, z_rows, hidden, grads, summed))
        active, x_rows, z_rows, hidden, grads, summed = zip(*packed)
        active = jnp.stack(active)
        grad_w_gate, grad_w_up = up_grads(active, x_rows, grads, 2)
        grad_w_down = down_grads(active, hidden, z_rows, 1)
        grad_x = (jnp.concatenate(summed, axis=0) + shared_dx).astype(BF16)
        return grad_x, grad_w_gate, grad_w_up, grad_w_down, grad_shared_gate, grad_shared_up, grad_shared_down

    return jax.shard_map(local_backward, mesh=mesh, in_specs=(token_spec, token_spec, token_spec, token_spec, token_spec, expert_spec, expert_spec, expert_spec, whole_spec, whole_spec, whole_spec), out_specs=(token_spec, grad_spec, grad_spec, grad_spec, grad_spec, grad_spec, grad_spec), check_vma=False)
```

time: 2900 us -> 1580 us (0.54)
  Pallas kernels: 0 us -> 1130 us
  matrix products: 1040 us -> 0.31 us
  local copies, waits for them, and re-layouts: 817 us -> 16.9 us
  waiting for transfers between devices: 882 us -> 353 us
  other arithmetic: 125 us -> 21.6 us
    pallas_call x0 -> x11, Pallas kernels: none -> 1130 us  [the longest x3 442 us: ffn_tiles(): pl.pallas_call(ffn_kernel, grid_spec=pltpu.PrefetchScalarGridSpec(num_sca...]
    dot_general x16 -> x2, matrix products: 1040 us -> 0.31 us  [chunk_tables(): jnp.dot(hit.reshape(-1, TB).astype(BF16), tri, preferred_element_type=F32)]
    all_to_all x3 -> x0, waiting for transfers between devices: 882 us -> none  [the longest x1 433 us: local_backward(): x_exp = lax.all_to_all(send_x, 'ep', 0, 1, tiled=True)]
    gather x4 -> x0, local copies, waits for them, and re-layouts: 486 us -> none  [take_rows(): return jnp.take(rows, row_index, axis=0, mode='fill', fill_value=0)]
    all_gather x0 -> x4, waiting for transfers between devices: none -> 212 us  [the longest x2 122 us: local_backward(): lax.all_gather(dy_tokens[rows], 'ep', axis=0, tiled=True)]
    reduce_scatter x0 -> x2, waiting for transfers between devices: none -> 139 us  [local_backward(): lax.psum_scatter(token_sums(lo, hi, pos, back), 'ep', scatter_dimension=0...]
    all_to_all x3 -> x0, local copies, waits for them, and re-layouts: 112 us -> none  [the longest x1 37.5 us: local_backward(): lax.all_to_all(grad_exp, 'ep', 1, 0, tiled=True)]
    convert_element_type x1 -> x0, local copies, waits for them, and re-layouts: 100 us -> none  [local_backward(): (jnp.einsum('erf,edf->erd', grad_gate, w_gate, preferred_element_type=jnp...]
  transfers between devices with their start and end apart: 3 -> 6, of which waited for: 3 -> 3; matrix products, arithmetic and copies ran while one was open for 33% -> 1% of each run, Pallas kernels for 0% -> 72%
where the time goes in v1:
time: 1580 us; the launch traced here: 1550 us
  Pallas kernels  1130 us (72%)
  waiting for transfers between devices  353 us (22%)
  blocking collectives  21.7 us (1%)
  other arithmetic  21.6 us (1%)
  local copies, waits for them, and re-layouts  16.9 us (1%)
    pallas_call x3, Pallas kernels, ffn_tiles(): pl.pallas_call(ffn_kernel, grid_spec=pltpu.PrefetchScalarGridSpec(num_sca...  442 us
    pallas_call x2, Pallas kernels, pack_rows(): pl.pallas_call(pack_kernel, grid_spec=pltpu.PrefetchScalarGridSpec(num_sc...  253 us
    pallas_call x2, Pallas kernels, up_grads(): pl.pallas_call(functools.partial(up_grad_kernel, chunks), grid_spec=pltpu...  222 us
    reduce_scatter x2, waiting for transfers between devices, local_backward(): lax.psum_scatter(token_sums(lo, hi, pos, back), 'ep', scatter_dimension=0...  139 us
    all_gather x2, waiting for transfers between devices, local_backward(): lax.all_gather(dy_tokens[rows], 'ep', axis=0, tiled=True)  122 us
    pallas_call x2, Pallas kernels, down_grads(): pl.pallas_call(functools.partial(down_grad_kernel, chunks), grid_spec=plt...  110 us
    pallas_call x2, Pallas kernels, token_sums(): pl.pallas_call(functools.partial(token_sum_kernel, experts), grid_spec=pl...  99 us
    all_gather x2, waiting for transfers between devices, local_backward(): lax.all_gather(x_tokens[rows], 'ep', axis=0, tiled=True)  90.3 us
  transfers between devices with their start and end apart: 6, of which 3 were waited for; matrix products, arithmetic and copies ran while one was open for 1% of the time, Pallas kernels for 72%

profile of v1, /device:TPU:0, one launch (start us, length us, event | category | flops | bytes accessed | tf_op | source)
XLA Modules:
  0.0 1554.6 jit_solution(8405643181459850683)
XLA Ops:
  7.2 6.7 fusion.16
  14.0 6.7 fusion.15
  20.7 0.7 all-gather.7.cloned.1.call-update
  22.1 21.7 %all-gather.1 = f32[8,12,1536]{2,1,0:T(8,128)S(1)} all-gather(f32[1,12,1536]{2,1,0:T(8,128)S(1)} %maximum_bitcast_fusion), channel_id=2, replica_groups=mesh['dp'=1,'ep'=8] {'ep'}, dimensions={0}, use_global_device_ids=true | all-gather | bytes 663552 | tf_op jit(solution)/shard_map/all_gather | solution.py:308
  44.8 1.0 fusion.1
  45.8 0.7 reshape.655.gate_ref
  46.8 0.7 select_reduce_fusion.1
  48.0 0.6 pad_add_fusion.3.tile_ref
  49.1 0.7 and_select_fusion.6
  49.8 0.6 broadcast_select_fusion.lo_ref
  50.4 0.8 add_select_fusion.pos_ref
  51.1 90.3 %all-gather.11.cloned.1.call-done.x_ref = bf16[6144,2048]{1,0:T(8,128)(2,1)} async-done(((bf16[768,2048]{1,0:T(8,128)(2,1)}), bf16[6144,2048]{1,0:T(8,128)(2,1)}) %all-gather.11.cloned.1.call-update) | async-done | bytes 25165840 | tf_op jit(solution)/shard_map/all_gather | solution.py:312
  141.5 122.1 %all-gather.13.cloned.1.call-done.dy_ref = bf16[6144,2048]{1,0:T(8,128)(2,1)} async-done(((bf16[768,2048]{1,0:T(8,128)(2,1)}), bf16[6144,2048]{1,0:T(8,128)(2,1)}) %all-gather.13.cloned.1.call-update) | async-done | bytes 25165840 | tf_op jit(solution)/shard_map/all_gather | solution.py:312
  263.5 126.5 %pack_rows.3 = (bf16[2,6144,2048]{2,1,0:T(8,128)(2,1)}, bf16[2,6144,2048]{2,1,0:T(8,128)(2,1)}) custom-call(s32[2,50]{1,0:T(2,128)} %pad_add_fusion.3.tile_ref, bf16[6144,2048]{1,0:T(8,128)(2,1)} %all-gather.11.cloned.1.call-done.x_ref, bf16[6144,2048]{1,0:T(8,128)(2,1)} %all-gather.13.cloned.1.call-done.dy_ref, s32[2,24,1,256]{3,2,1,0:T(1,128)} %add_select_fusion.pos_ref, ...), custom_call_target="tpu_custom_call" | custom-call | flops 30000001024 | bytes 200000000 | tf_op jit(solution)/shard_map/pack_rows/pallas_call | solution.py:70
  390.0 166.0 %ffn_tiles.3 = (bf16[2,6144,1408]{2,1,0:T(8,128)(2,1)}, bf16[2,6144,2816]{2,1,0:T(8,128)(2,1)}, bf16[2,6144,2048]{2,1,0:T(8,128)(2,1)}) custom-call(s32[2]{0:T(128)} %fusion.11.n_ref, bf16[2,6144,2048]{2,1,0:T(8,128)(2,1)} %get-tuple-element.31.x_ref.refs_1_, bf16[2,6144,2048]{2,1,0:T(8,128)(2,1)} %get-tuple-element.32.z_ref.refs_3_, ...), custom_call_target="tpu_custom_call" | custom-call | flops 88583700480 | bytes 150000000 | tf_op jit(solution)/shard_map/ffn_tiles/pallas_call | solution.py:113
  556.0 50.1 %token_sums.3 = f32[6144,2048]{1,0:T(8,128)} custom-call(s32[2,24]{1,0:T(2,128)} %broadcast_select_fusion.lo_ref, s32[2,24]{1,0:T(2,128)} %get-tuple-element.53.hi_ref, s32[2,24,1,256]{3,2,1,0:T(1,128)} %add_select_fusion.pos_ref, bf16[2,6144,2048]{2,1,0:T(8,128)(2,1)} %get-tuple-element.33.refs_0_.refs_1_.refs_2_.refs_3_, ...), custom_call_target="tpu_custom_call" | custom-call | flops 20000000000 | bytes 100000000 | tf_op jit(solution)/shard_map/token_sums/pallas_call | solution.py:248
  606.2 0.6 copy-done.1
  607.0 0.7 reshape.651.gate_ref
  608.4 0.7 pad_add_fusion.2.tile_ref
  609.6 0.6 and_select_fusion.14
  610.8 0.7 add_select_fusion.1.pos_ref
  611.5 109.4 %shared_ffn.1 = (bf16[1,1536,2816]{2,1,0:T(8,128)(2,1)}, bf16[1,1536,5632]{2,1,0:T(8,128)(2,1)}, f32[1,1536,2048]{2,1,0:T(8,128)}) custom-call(s32[1]{0:T(128)} %constant.114.clone.1.n_ref, bf16[1,1536,2048]{2,1,0:T(8,128)(2,1)} %bitcast.92, bf16[1,1536,2048]{2,1,0:T(8,128)(2,1)} %bitcast.90, bf16[1,2048,2816]{2,1,0:T(8,128)(2,1)} %bitcast.103, ...), custom_call_target="tpu_custom_call" | custom-call | flops 44291850240 | bytes 150000000 | tf_op jit(solution)/shard_map/shared_ffn/pallas_call | solution.py:113
  721.0 28.7 %down_grads.2.refs_2_ = f32[1,2816,2048]{2,1,0:T(8,128)} custom-call(s32[1,1]{1,0:T(1,128)} %constant.113.clone.1.n_ref, bf16[1,1536,2816]{2,1,0:T(8,128)(2,1)} %get-tuple-element.27.refs_0_, bf16[1,1536,2048]{2,1,0:T(8,128)(2,1)} %bitcast.91), custom_call_target="tpu_custom_call" | custom-call | flops 60000002048 | bytes 150000000 | tf_op jit(solution)/shard_map/down_grads/pallas_call | solution.py:215
  749.7 57.5 %up_grads.2 = (f32[1,2048,2816]{2,1,0:T(8,128)}, f32[1,2048,2816]{2,1,0:T(8,128)}) custom-call(s32[1,1]{1,0:T(1,128)} %constant.113.clone.1.n_ref, bf16[1,1536,2048]{2,1,0:T(8,128)(2,1)} %bitcast.93, bf16[1,1536,5632]{2,1,0:T(8,128)(2,1)} %get-tuple-element.24.refs_1_), custom_call_target="tpu_custom_call" | custom-call | flops 120000004096 | bytes 250000000 | tf_op jit(solution)/shard_map/up_grads/pallas_call | solution.py:181
  807.1 126.8 %pack_rows.2 = (bf16[2,6144,2048]{2,1,0:T(8,128)(2,1)}, bf16[2,6144,2048]{2,1,0:T(8,128)(2,1)}) custom-call(s32[2,50]{1,0:T(2,128)} %pad_add_fusion.2.tile_ref, bf16[6144,2048]{1,0:T(8,128)(2,1)} %all-gather.7.cloned.1.call-done.x_ref, bf16[6144,2048]{1,0:T(8,128)(2,1)} %all-gather.9.cloned.1.call-done.dy_ref, s32[2,24,1,256]{3,2,1,0:T(1,128)} %add_select_fusion.1.pos_ref, ...), custom_call_target="tpu_custom_call" | custom-call | flops 30000001024 | bytes 200000000 | tf_op jit(solution)/shard_map/pack_rows/pallas_call | solution.py:70
  934.0 166.2 %ffn_tiles.2 = (bf16[2,6144,1408]{2,1,0:T(8,128)(2,1)}, bf16[2,6144,2816]{2,1,0:T(8,128)(2,1)}, bf16[2,6144,2048]{2,1,0:T(8,128)(2,1)}) custom-call(s32[2]{0:T(128)} %fusion.12.n_ref, bf16[2,6144,2048]{2,1,0:T(8,128)(2,1)} %get-tuple-element.28.x_ref.refs_0_, bf16[2,6144,2048]{2,1,0:T(8,128)(2,1)} %get-tuple-element.29.z_ref.refs_2_, ...), custom_call_target="tpu_custom_call" | custom-call | flops 88583700480 | bytes 150000000 | tf_op jit(solution)/shard_map/ffn_tiles/pallas_call | solution.py:113
  1100.1 48.9 %token_sums.2 = f32[6144,2048]{1,0:T(8,128)} custom-call(s32[2,24]{1,0:T(2,128)} %broadcast_select_fusion.1.lo_ref, s32[2,24]{1,0:T(2,128)} %get-tuple-element.51.hi_ref, s32[2,24,1,256]{3,2,1,0:T(1,128)} %add_select_fusion.1.pos_ref, bf16[2,6144,2048]{2,1,0:T(8,128)(2,1)} %get-tuple-element.30.refs_0_.refs_1_.refs_2_.refs_3_, ...), custom_call_target="tpu_custom_call" | custom-call | flops 20000000000 | bytes 100000000 | tf_op jit(solution)/shard_map/token_sums/pallas_call | solution.py:248
  1149.0 0.6 copy-done.12
  1150.3 81.1 %down_grads.3 = f32[2,1408,2048]{2,1,0:T(8,128)} custom-call(s32[2,2]{1,0:T(2,128)} %pad_add_fusion.4.n_ref, bf16[2,6144,1408]{2,1,0:T(8,128)(2,1)} %get-tuple-element.39.refs_0_, bf16[2,6144,1408]{2,1,0:T(8,128)(2,1)} %get-tuple-element.40.refs_1_, bf16[2,6144,2048]{2,1,0:T(8,128)(2,1)} %get-tuple-element.29.z_ref.refs_2_, ...), custom_call_target="tpu_custom_call" | custom-call | flops 60000002048 | bytes 150000000 | tf_op jit(solution)/shard_map/down_grads/pallas_call | solution.py:215
  1231.3 165.0 %up_grads.3 = (f32[2,2048,1408]{2,1,0:T(8,128)}, f32[2,2048,1408]{2,1,0:T(8,128)}) custom-call(s32[2,2]{1,0:T(2,128)} %pad_add_fusion.4.n_ref, bf16[2,6144,2048]{2,1,0:T(8,128)(2,1)} %get-tuple-element.28.x_ref.refs_0_, bf16[2,6144,2048]{2,1,0:T(8,128)(2,1)} %get-tuple-element.31.x_ref.refs_1_, bf16[2,6144,2816]{2,1,0:T(8,128)(2,1)} %get-tuple-element.35.refs_2_, ...), custom_call_target="tpu_custom_call" | custom-call | flops 120000004096 | bytes 250000000 | tf_op jit(solution)/shard_map/up_grads/pallas_call | solution.py:181
  1396.3 139.2 %reduce-scatter.3.cloned.1.call-done = f32[768,2048]{1,0:T(8,128)} async-done(((f32[6144,2048]{1,0:T(8,128)}), f32[768,2048]{1,0:T(8,128)}) %reduce-scatter.3.cloned.1.call-update) | async-done | bytes 6291472 | tf_op jit(solution)/shard_map/reduce_scatter | solution.py:321
  1535.6 11.7 fusion
  (73 shorter events, 5.6 us)
Async XLA Ops:
  7.2 134.3 %all-gather.11.cloned.1.call-start = ((), (), s32[]{:S(2)}) async-start(), calls=%async_computation.5 | async-start | bytes 28311552 | tf_op jit(solution)/shard_map/all_gather | solution.py:312
  13.9 8.2 copy-start.3
  13.9 8.2 copy-start.4
  13.9 8.2 copy-start.5
  13.9 249.6 %all-gather.13.cloned.1.call-start = ((), (), s32[]{:S(2)}) async-start(), calls=%async_computation.6 | async-start | bytes 28311552 | tf_op jit(solution)/shard_map/all_gather | solution.py:312
  20.7 786.5 %all-gather.7.cloned.1.call-start = ((), (), s32[]{:S(2)}) async-start(), calls=%async_computation.2 | async-start | bytes 28311552 | tf_op jit(solution)/shard_map/all_gather | solution.py:312
  21.4 785.7 %all-gather.9.cloned.1.call-start = ((), (), s32[]{:S(2)}) async-start(), calls=%async_computation.3 | async-start | bytes 28311552 | tf_op jit(solution)/shard_map/all_gather | solution.py:312
  22.0 1374.4 %reduce-scatter.5.cloned.1.call-start = ((), (), s32[]{:S(2)}) async-start(), calls=%async_computation.7 | async-start | bytes 56623104 | tf_op jit(solution)/shard_map/reduce_scatter | solution.py:321
  44.4 2.1 copy-start
  46.7 1.1 copy-start.6
  47.7 3.4 copy-start.9
  606.1 0.7 copy-start.1
  606.1 0.8 copy-start.2
  606.1 1.8 copy-start.7
  606.1 1.8 copy-start.8
  606.2 929.4 %reduce-scatter.3.cloned.1.call-start = ((), (), s32[]{:S(2)}) async-start(), calls=%async_computation.4 | async-start | bytes 56623104 | tf_op jit(solution)/shard_map/reduce_scatter | solution.py:321
  608.1 3.4 copy-start.11
  1149.0 0.6 copy-start.12
  1149.0 0.7 copy-start.10
Sparse Core Ops, SparseCore 0:
  14.0 127.3 all-gather.10
  143.8 119.6 all-gather.12
  265.9 119.6 all-gather.6
  387.8 119.6 all-gather.8
  606.3 315.5 reduce-scatter.4
  1149.2 386.3 reduce-scatter.2

commit v2 on v1

v2 whole, which is shorter than its diff:
```python
import functools

import jax
import jax.numpy as jnp
from jax import lax
from jax.experimental import pallas as pl
from jax.experimental.pallas import tpu as pltpu
from jax.sharding import PartitionSpec as P

BF16, F32, I32 = jnp.bfloat16, jnp.float32, jnp.int32
TB = 256
TM = 512
WINDOW = 768
CHUNKS = 3
VMEM = 64 * 1024 * 1024 - 128 * 1024


def dot(a, b):
    return lax.dot_general(a, b, (((1,), (0,)), ((), ())), preferred_element_type=F32)


def dot_t(a, b):
    return lax.dot_general(a, b, (((1,), (1,)), ((), ())), preferred_element_type=F32)


def params(ndim):
    return pltpu.CompilerParams(dimension_semantics=("arbitrary",) * ndim, vmem_limit_bytes=VMEM)


def swiglu_parts(act_gate, act_up, grad_hidden):
    gate_f32 = act_gate.astype(F32)
    up_f32 = act_up.astype(F32)
    sigma = jax.nn.sigmoid(gate_f32)
    silu_gate = gate_f32 * sigma
    hidden = (silu_gate * up_f32).astype(BF16)
    grad_gate = (grad_hidden * up_f32 * sigma * (1.0 + gate_f32 * (1.0 - sigma))).astype(BF16)
    grad_up = (grad_hidden * silu_gate).astype(BF16)
    return hidden, grad_gate, grad_up


def pack_kernel(first_ref, window_ref, n_ref, x_ref, dy_ref, pos_ref, gate_ref, *refs):
    xo_ref, zo_ref = refs[-2:]
    e, m = pl.program_id(0), pl.program_id(1)
    tokens = x_ref.shape[0]

    def window(w):
        wanted = first_ref[e, m] + w * WINDOW
        begin = pl.multiple_of(jnp.minimum(wanted, tokens - WINDOW), 128)
        at = pl.ds(begin, WINDOW)
        token = begin + lax.broadcasted_iota(I32, (1, WINDOW), 1)
        local = jnp.where(token >= wanted, pos_ref[0, :, at] - m * TB, -1)
        hit = lax.broadcasted_iota(I32, (TB, WINDOW), 0) == local
        row_gate = jnp.sum(jnp.where(hit, gate_ref[0, :, at], 0.0), axis=1, keepdims=True)
        pick = hit.astype(F32).astype(BF16)
        return dot(pick, x_ref[at, :]).astype(BF16), (dot(pick, dy_ref[at, :]) * row_gate).astype(BF16)

    @pl.when(m < n_ref[e])
    def _():
        xo_ref[0], zo_ref[0] = window(0)

    def more(w, carry):
        x_rows, z_rows = window(w)
        xo_ref[0] += x_rows
        zo_ref[0] += z_rows
        return carry

    lax.fori_loop(1, jnp.where(m < n_ref[e], window_ref[e, m], 1), more, 0)


def pack_rows(first, windows, units, x, dy, pos, gate, chunk, held, after):
    experts = pos.shape[0]
    rows, dim = x.shape
    tok = pl.BlockSpec((rows, dim), lambda e, m, f, w, n: (0, 0), pipeline_mode=pl.Buffered(1))
    row = pl.BlockSpec((1, 1, rows), lambda e, m, f, w, n: (e, 0, 0))
    out = pl.BlockSpec((1, TB, dim), lambda e, m, f, w, n: (e, chunk * (rows // TB) + jnp.minimum(m, n[e] - 1), 0))
    return pl.pallas_call(
        pack_kernel,
        grid_spec=pltpu.PrefetchScalarGridSpec(
            num_scalar_prefetch=3, grid=(experts, rows // TB),
            in_specs=[tok, tok, row, row] + [pl.BlockSpec(memory_space=pl.ANY)] * (len(held) + len(after)),
            out_specs=[out, out]),
        out_shape=[jax.ShapeDtypeStruct((experts, CHUNKS * rows, dim), BF16)] * 2,
        input_output_aliases={7 + i: i for i in range(len(held))},
        compiler_params=params(2),
        cost_estimate=pl.CostEstimate(flops=30_000_000_000, bytes_accessed=200_000_000, transcendentals=0),
        name="pack_rows",
    )(first, windows, units, x, dy, pos, gate, *held, *after)


def ffn_kernel(sizes, n_ref, x_ref, z_ref, w1_ref, w3_ref, w2_ref, *refs):
    h_ref, d_ref, r_ref = refs[-3:]
    ff = w1_ref.shape[2]
    dim = w1_ref.shape[1]
    left = n_ref[pl.program_id(0)] - len(sizes) * pl.program_id(1)

    def tile(rows):
        def columns(lo, size, act_gate, act_up):
            grad_hidden = dot_t(z_ref[0, :rows], w2_ref[0, lo:lo + size, :])
            hidden, grad_gate, grad_up = swiglu_parts(act_gate.astype(BF16), act_up.astype(BF16), grad_hidden)
            h_ref[0, :rows, lo:lo + size] = hidden
            d_ref[0, :rows, lo:lo + size] = grad_gate
            d_ref[0, :rows, ff + lo:ff + lo + size] = grad_up

        full = ff // 256 * 256
        for lo in range(0, full, 256):
            columns(lo, 256, dot(x_ref[0, :rows], w1_ref[0, :, lo:lo + 256]), dot(x_ref[0, :rows], w3_ref[0, :, lo:lo + 256]))
        if full < ff:
            both = dot(x_ref[0, :rows], jnp.concatenate([w1_ref[0, :, full:], w3_ref[0, :, full:]], axis=1))
            columns(full, ff - full, both[:, :ff - full], both[:, ff - full:])
        for lo in range(0, dim, 256):
            w = jnp.concatenate([w1_ref[0, lo:lo + 256, :], w3_ref[0, lo:lo + 256, :]], axis=1)
            r_ref[0, :rows, lo:lo + 256] = dot_t(d_ref[0, :rows], w).astype(r_ref.dtype)

    for i, rows in enumerate(sizes):
        pl.when((left == i + 1) if i + 1 < len(sizes) else (left > i))(functools.partial(tile, rows))


def ffn_tiles(units, x, z, w1, w3, w2, out_dtype, sizes, chunks, chunk, held, name):
    experts, dim, ff = w1.shape
    rows = x.shape[1] // chunks
    tm, per = sizes[-1], len(sizes)
    inner = lambda e, m, n: jnp.minimum(m, (n[e] + per - 1) // per - 1)
    tile = lambda e, m, n: (e, chunk * (rows // tm) + inner(e, m, n), 0)
    whole = lambda e, m, n: (e, 0, 0)
    return pl.pallas_call(
        functools.partial(ffn_kernel, sizes),
        grid_spec=pltpu.PrefetchScalarGridSpec(
            num_scalar_prefetch=1, grid=(experts, rows // tm),
            in_specs=[pl.BlockSpec((1, tm, dim), tile), pl.BlockSpec((1, tm, dim), tile),
                      pl.BlockSpec((1, dim, ff), whole, pipeline_mode=pl.Buffered(1)),
                      pl.BlockSpec((1, dim, ff), whole, pipeline_mode=pl.Buffered(1)),
                      pl.BlockSpec((1, ff, dim), whole, pipeline_mode=pl.Buffered(1))] + [pl.BlockSpec(memory_space=pl.ANY)] * len(held),
            out_specs=[pl.BlockSpec((1, tm, ff), tile), pl.BlockSpec((1, tm, 2 * ff), tile),
                       pl.BlockSpec((1, tm, dim), lambda e, m, n: (e, inner(e, m, n), 0))]),
        out_shape=[jax.ShapeDtypeStruct((experts, chunks * rows, ff), BF16),
                   jax.ShapeDtypeStruct((experts, chunks * rows, 2 * ff), BF16),
                   jax.ShapeDtypeStruct((experts, rows, dim), out_dtype)],
        input_output_aliases={6 + i: i for i in range(len(held))},
        compiler_params=params(2),
        cost_estimate=pl.CostEstimate(flops=5 * experts * rows * dim * ff, bytes_accessed=150_000_000, transcendentals=0),
        name=name,
    )(units, x, z, w1, w3, w2, *held)


def for_tile(sizes, left_ref, body):
    left = left_ref[pl.program_id(0), pl.program_id(2)]
    for i, rows in enumerate(sizes):
        pl.when((left == i + 1) if i + 1 < len(sizes) else (left > i))(functools.partial(body, rows))


def up_grad_kernel(sizes, tile_ref, left_ref, x_ref, d_ref, g1_ref, g3_ref):
    ff = g1_ref.shape[2]

    @pl.when(pl.program_id(2) == 0)
    def _():
        g1_ref[...] = jnp.zeros_like(g1_ref)
        g3_ref[...] = jnp.zeros_like(g3_ref)

    def body(rows):
        x_t = x_ref[0, :rows].T
        for lo in range(0, 2 * ff, 256):
            part = dot(x_t, d_ref[0, :rows, lo:lo + 256])
            if lo + 256 <= ff:
                g1_ref[0, :, lo:lo + 256] += part
            elif lo >= ff:
                g3_ref[0, :, lo - ff:lo - ff + 256] += part
            else:
                g1_ref[0, :, lo:] += part[:, :ff - lo]
                g3_ref[0, :, :lo + 256 - ff] += part[:, ff - lo:]

    for_tile(sizes, left_ref, body)


def up_grads(tiles, left, x, d, split, sizes):
    experts, _, dim = x.shape
    ff = d.shape[2] // 2
    out = lambda e, s, j, t, n: (e, s, 0)
    return pl.pallas_call(
        functools.partial(up_grad_kernel, sizes),
        grid_spec=pltpu.PrefetchScalarGridSpec(
            num_scalar_prefetch=2, grid=(experts, split, tiles.shape[1]),
            in_specs=[pl.BlockSpec((1, TM, dim // split), lambda e, s, j, t, n: (e, t[e, j], s)),
                      pl.BlockSpec((1, TM, 2 * ff), lambda e, s, j, t, n: (e, t[e, j], 0))],
            out_specs=[pl.BlockSpec((1, dim // split, ff), out)] * 2),
        out_shape=[jax.ShapeDtypeStruct((experts, dim, ff), F32)] * 2,
        compiler_params=params(3),
        cost_estimate=pl.CostEstimate(flops=120_000_000_000, bytes_accessed=250_000_000, transcendentals=0),
        name="up_grads",
    )(tiles, left, x, d)


def down_grad_kernel(sizes, tile_ref, left_ref, h_ref, z_ref, g_ref):
    @pl.when(pl.program_id(2) == 0)
    def _():
        g_ref[...] = jnp.zeros_like(g_ref)

    def body(rows):
        h_t = h_ref[0, :rows].T
        for lo in range(0, g_ref.shape[2], 256):
            g_ref[0, :, lo:lo + 256] += dot(h_t, z_ref[0, :rows, lo:lo + 256])

    for_tile(sizes, left_ref, body)


def down_grads(tiles, left, h, z, split, sizes):
    experts, _, ff = h.shape
    dim = z.shape[2]
    return pl.pallas_call(
        functools.partial(down_grad_kernel, sizes),
        grid_spec=pltpu.PrefetchScalarGridSpec(
            num_scalar_prefetch=2, grid=(experts, split, tiles.shape[1]),
            in_specs=[pl.BlockSpec((1, TM, ff), lambda e, s, j, t, n: (e, t[e, j], 0)),
                      pl.BlockSpec((1, TM, dim // split), lambda e, s, j, t, n: (e, t[e, j], s))],
            out_specs=[pl.BlockSpec((1, ff, dim // split), lambda e, s, j, t, n: (e, 0, s))]),
        out_shape=[jax.ShapeDtypeStruct((experts, ff, dim), F32)],
        compiler_params=params(3),
        cost_estimate=pl.CostEstimate(flops=60_000_000_000, bytes_accessed=150_000_000, transcendentals=0),
        name="down_grads",
    )(tiles, left, h, z)[0]


def gradient_tiles(units, chunk_tiles, steps):
    per = TM // TB
    tiles = (units + per - 1) // per
    ends = jnp.cumsum(tiles, axis=0)
    j = jnp.arange(steps, dtype=I32)
    j_in = jnp.minimum(j[None, :], ends[-1][:, None] - 1)
    chunk = jnp.sum((j_in[None] >= ends[:, :, None]).astype(I32), axis=0)
    begin = jnp.sum(jnp.where(jnp.arange(len(units))[:, None, None] < chunk[None], tiles[:, :, None], 0), axis=0)
    count = jnp.sum(jnp.where(jnp.arange(len(units))[:, None, None] == chunk[None], units[:, :, None], 0), axis=0)
    inner = j_in - begin
    left = jnp.where(j[None, :] < ends[-1][:, None], count - per * inner, 0)
    return (chunk * chunk_tiles + inner).astype(I32), left.astype(I32)


def token_sum_kernel(experts, lo_ref, hi_ref, pos_ref, *refs):
    b = pl.program_id(0)
    out_ref = refs[-1]
    picks, rows = [], []
    for e in range(experts):
        for near in range(2):
            tile = hi_ref[e, b] if near else lo_ref[e, b]
            local = pos_ref[e, 0] - tile * TB
            if near:
                local = jnp.where(tile == lo_ref[e, b], -1, local)
            picks.append((lax.broadcasted_iota(I32, (TB, TB), 0) == local).astype(F32).T.astype(BF16))
            rows.append(refs[2 * e + near][0])
    out_ref[...] = dot(jnp.concatenate(picks, axis=1), jnp.concatenate(rows, axis=0))


def token_sums(lo, hi, pos, r):
    experts, blocks = pos.shape[:2]
    dim = r.shape[2]
    specs = []
    for e in range(experts):
        specs.append(pl.BlockSpec((1, TB, dim), lambda b, l, h, e=e: (e, l[e, b], 0)))
        specs.append(pl.BlockSpec((1, TB, dim), lambda b, l, h, e=e: (e, h[e, b], 0)))
    return pl.pallas_call(
        functools.partial(token_sum_kernel, experts),
        grid_spec=pltpu.PrefetchScalarGridSpec(
            num_scalar_prefetch=2, grid=(blocks,),
            in_specs=[pl.BlockSpec((experts, 1, 1, TB), lambda b, l, h: (0, b, 0, 0))] + specs,
            out_specs=[pl.BlockSpec((TB, dim), lambda b, l, h: (b, 0))]),
        out_shape=[jax.ShapeDtypeStruct((blocks * TB, dim), F32)],
        compiler_params=params(1),
        cost_estimate=pl.CostEstimate(flops=20_000_000_000, bytes_accessed=100_000_000, transcendentals=0),
        name="token_sums",
    )(lo, hi, pos, *([r] * (2 * experts)))[0]


def shared_backward(x, dy, gate_w, up_w, down_w):
    x, dy = x[None], dy[None]
    tokens = x.shape[1]
    tm = tokens // 4
    tiles = jnp.arange(tokens // TM, dtype=I32)[None]
    ones = jnp.ones_like(tiles)
    hidden, grads, back = ffn_tiles(jnp.full((1,), 4, I32), x, dy, gate_w[None], up_w[None], down_w[None], F32, (tm,), 1, 0, (), "shared_ffn")
    grad_gate, grad_up = up_grads(tiles, ones, x, grads, 4, (TM,))
    grad_down = down_grads(tiles, ones, hidden, dy, 2, (TM,))
    return back[0], grad_gate, grad_up, grad_down


def chunk_tables(codes, gates, experts):
    top_k, tokens = codes.shape
    blocks = tokens // TB
    ids = lax.axis_index('ep') * experts + jnp.arange(experts, dtype=I32)
    match = codes[None] == ids[:, None, None].astype(F32)
    hit = jnp.any(match, axis=1).reshape(experts, blocks, TB)
    gate = jnp.sum(jnp.where(match, gates[None], 0.0), axis=1).reshape(experts, blocks, 1, TB)
    tri = (jnp.arange(TB)[:, None] < jnp.arange(TB)[None, :]).astype(BF16)
    rank = jnp.dot(hit.reshape(-1, TB).astype(BF16), tri, preferred_element_type=F32).astype(I32).reshape(experts, blocks, TB)
    count = jnp.sum(hit.astype(I32), axis=2)
    below = jnp.arange(blocks)[:, None] < jnp.arange(blocks)[None, :]
    start = jnp.sum(jnp.where(below[None], count[:, :, None], 0), axis=1)
    total = start[:, -1] + count[:, -1]
    pos = jnp.where(hit, start[:, :, None] + rank, -(1 << 20)).reshape(experts, blocks, 1, TB)
    units = jnp.maximum((total + TB - 1) // TB, 1)
    lo = jnp.minimum(start // TB, units[:, None] - 1)
    hi = jnp.minimum(lo + 1, units[:, None] - 1)
    fine = jnp.sum(hit.reshape(experts, tokens // 128, 128).astype(I32), axis=2)
    spans = tokens // 128
    fine_start = jnp.sum(jnp.where((jnp.arange(spans)[:, None] < jnp.arange(spans)[None, :])[None], fine[:, :, None], 0), axis=1)
    edge = jnp.arange(blocks, dtype=I32)[None, :, None] * TB
    first = jnp.sum((fine_start + fine)[:, None, :] <= edge, axis=2).astype(I32)
    inside = (fine_start[:, None, :] < edge + TB) & (fine_start < total[:, None])[:, None, :]
    last = jnp.sum(inside, axis=2).astype(I32) - 1
    windows = jnp.maximum(((last - first + 1) * 128 + WINDOW - 1) // WINDOW, 1)
    return first * 128, windows, units, lo, hi, pos, gate


def solution(mesh):
    group = mesh.shape['ep']
    token_spec = P(('dp', 'ep'), None)
    expert_spec = P('ep', None, None)
    whole_spec = P(None, None)
    grad_spec = P(('dp', 'ep'), None, None)

    def local_backward(x_tokens, dy_tokens, expert_ids, gate_vals, slot_pos, w_gate, w_up, w_down, shared_gate, shared_up, shared_down):
        tok_count, top_k = expert_ids.shape
        local_experts = w_gate.shape[0]
        part = tok_count // CHUNKS
        codes = jnp.where(slot_pos >= 0, expert_ids, -1).astype(F32).T
        plan = lax.all_gather(jnp.concatenate([codes, gate_vals.T], axis=0), 'ep', axis=0)
        gathered = []
        for c in range(CHUNKS):
            rows = slice(c * part, (c + 1) * part)
            gathered.append((lax.all_gather(x_tokens[rows], 'ep', axis=0, tiled=True), lax.all_gather(dy_tokens[rows], 'ep', axis=0, tiled=True)))
        shared = shared_backward(x_tokens, dy_tokens, shared_gate, shared_up, shared_down)
        shared_dx, grad_shared_gate, grad_shared_up, grad_shared_down = shared
        packed, wide, summed, units, after = (), (), [], [], shared[1:]
        for c in range(CHUNKS):
            mine = plan[:, :, c * part:(c + 1) * part].transpose(1, 0, 2).reshape(2 * top_k, group * part)
            first, windows, count, lo, hi, pos, gate = chunk_tables(mine[:top_k], mine[top_k:], local_experts)
            packed = pack_rows(first, windows, count, *gathered[c], pos.reshape(local_experts, 1, -1), gate.reshape(local_experts, 1, -1), c, packed, after)
            *wide, back = ffn_tiles(count, *packed, w_gate, w_up, w_down, BF16, (TB, TM), CHUNKS, c, wide, "ffn_tiles")
            sums = token_sums(lo, hi, pos, back)
            after = (sums,)
            summed.append(lax.psum_scatter(sums, 'ep', scatter_dimension=0, tiled=True))
            units.append(count)
        capacity = (3 * tok_count * top_k + 2 * local_experts * group - 1) // (2 * local_experts * group)
        steps = min(CHUNKS * group * part // TM, (group * capacity + CHUNKS * (TM - 1)) // TM)
        tiles, left = gradient_tiles(jnp.stack(units), group * part // TM, steps)
        x_rows, z_rows = packed
        hidden, grads = wide
        grad_w_gate, grad_w_up = up_grads(tiles, left, x_rows, grads, 2, (TB, TM))
        grad_w_down = down_grads(tiles, left, hidden, z_rows, 1, (TB, TM))
        grad_x = (jnp.concatenate(summed, axis=0) + shared_dx).astype(BF16)
        return grad_x, grad_w_gate, grad_w_up, grad_w_down, grad_shared_gate, grad_shared_up, grad_shared_down

    return jax.shard_map(local_backward, mesh=mesh, in_specs=(token_spec, token_spec, token_spec, token_spec, token_spec, expert_spec, expert_spec, expert_spec, whole_spec, whole_spec, whole_spec), out_specs=(token_spec, grad_spec, grad_spec, grad_spec, grad_spec, grad_spec, grad_spec), check_vma=False)
```

time: 1580 us -> 1220 us (0.77)
  the two profiles are of different devices: /device:TPU:0 before, /device:TPU:3 now
where the time goes in v2:
time: 1220 us; the launch traced here: 1200 us
  Pallas kernels  1110 us (91%)
  other arithmetic  36.8 us (3%)
  local copies, waits for them, and re-layouts  20.3 us (2%)
  blocking collectives  18 us (1%)
  between operations  14.5 us (1%)
    pallas_call x4, Pallas kernels, ffn_tiles(): pl.pallas_call(functools.partial(ffn_kernel, sizes), grid_spec=pltpu.Pref...  522 us
    pallas_call x2, Pallas kernels, up_grads(): pl.pallas_call(functools.partial(up_grad_kernel, sizes), grid_spec=pltpu....  229 us
    pallas_call x3, Pallas kernels, pack_rows(): pl.pallas_call(pack_kernel, grid_spec=pltpu.PrefetchScalarGridSpec(num_sc...  135 us
    pallas_call x2, Pallas kernels, down_grads(): pl.pallas_call(functools.partial(down_grad_kernel, sizes), grid_spec=pltp...  114 us
    pallas_call x3, Pallas kernels, token_sums(): pl.pallas_call(functools.partial(token_sum_kernel, experts), grid_spec=pl...  105 us
  transfers between devices with their start and end apart: 9, of which 0 were waited for; matrix products, arithmetic and copies ran while one was open for 3% of the time, Pallas kernels for 92%

profile of v2, /device:TPU:3, one launch (start us, length us, event | category | flops | bytes accessed | tf_op | source)
XLA Modules:
  0.0 1198.5 jit_solution(8285351478432682584)
XLA Ops:
  7.2 5.8 fusion.28
  13.1 5.8 fusion.27
  22.7 18.0 %all-gather.1 = f32[8,12,1536]{2,1,0:T(8,128)S(1)} all-gather(f32[1,12,1536]{2,1,0:T(8,128)S(1)} %maximum_bitcast_fusion), channel_id=2, replica_groups=mesh['dp'=1,'ep'=8] {'ep'}, dimensions={0}, use_global_device_ids=true | all-gather | bytes 663552 | tf_op jit(solution)/shard_map/all_gather | solution.py:323
  42.9 1.0 fusion.1
  47.8 0.8 fusion.23
  49.2 0.8 add_reduce_fusion.1
  50.7 109.4 %shared_ffn.1 = (bf16[1,1536,2816]{2,1,0:T(8,128)(2,1)}, bf16[1,1536,5632]{2,1,0:T(8,128)(2,1)}, f32[1,1536,2048]{2,1,0:T(8,128)}) custom-call(s32[1]{0:T(128)} %constant.137.clone.1.n_ref, bf16[1,1536,2048]{2,1,0:T(8,128)(2,1)} %bitcast.87, bf16[1,1536,2048]{2,1,0:T(8,128)(2,1)} %bitcast.85, bf16[1,2048,2816]{2,1,0:T(8,128)(2,1)} %bitcast.105, ...), custom_call_target="tpu_custom_call" | custom-call | flops 44291850240 | bytes 150000000 | tf_op jit(solution)/shard_map/shared_ffn/pallas_call | solution.py:125
  161.3 29.4 %down_grads.2.refs_2_ = f32[1,2816,2048]{2,1,0:T(8,128)} custom-call(s32[1,3]{1,0:T(1,128)} %iota.96.tile_ref, s32[1,3]{1,0:T(1,128)} %broadcast_27_left_ref.2.left_ref, bf16[1,1536,2816]{2,1,0:T(8,128)(2,1)} %get-tuple-element.32.h_ref, bf16[1,1536,2048]{2,1,0:T(8,128)(2,1)} %bitcast.86), custom_call_target="tpu_custom_call" | custom-call | flops 60000002048 | bytes 150000000 | tf_op jit(solution)/shard_map/down_grads/pallas_call | solution.py:208
  190.6 1.5 convert_reduce_fusion.5
  192.8 0.8 broadcast_compare_fusion.2
  193.6 1.5 convert_reduce_fusion.4
  195.1 1.1 fusion.20.n_ref
  196.2 1.3 add_minimum_fusion.2
  198.1 1.5 add_select_fusion.2.pos_ref
  199.6 1.4 copy_select_fusion.2.pos_ref
  201.5 58.2 %up_grads.2 = (f32[1,2048,2816]{2,1,0:T(8,128)}, f32[1,2048,2816]{2,1,0:T(8,128)}) custom-call(s32[1,3]{1,0:T(1,128)} %iota.95.tile_ref, s32[1,3]{1,0:T(1,128)} %broadcast_27_left_ref.2.left_ref, bf16[1,1536,2048]{2,1,0:T(8,128)(2,1)} %bitcast.88, bf16[1,1536,5632]{2,1,0:T(8,128)(2,1)} %get-tuple-element.29.d_ref), custom_call_target="tpu_custom_call" | custom-call | flops 120000004096 | bytes 250000000 | tf_op jit(solution)/shard_map/up_grads/pallas_call | solution.py:178
  259.8 43.9 %pack_rows.3 = (bf16[2,12288,2048]{2,1,0:T(8,128)(2,1)}, bf16[2,12288,2048]{2,1,0:T(8,128)(2,1)}) custom-call(s32[2,16]{1,0:T(2,128)} %get-tuple-element.112.first_ref, s32[2,16]{1,0:T(2,128)} %get-tuple-element.111.window_ref, s32[2]{0:T(128)} %fusion.20.n_ref, bf16[4096,2048]{1,0:T(8,128)(2,1)} %all-gather.9.cloned.1.call-done.x_ref, ...), custom_call_target="tpu_custom_call" | custom-call | flops 30000001024 | bytes 200000000 | tf_op jit(solution)/shard_map/pack_rows/pallas_call | solution.py:76
  303.7 127.2 %ffn_tiles.3 = (bf16[2,12288,1408]{2,1,0:T(8,128)(2,1)}, bf16[2,12288,2816]{2,1,0:T(8,128)(2,1)}, bf16[2,4096,2048]{2,1,0:T(8,128)(2,1)}) custom-call(s32[2]{0:T(128)} %fusion.20.n_ref, bf16[2,12288,2048]{2,1,0:T(8,128)(2,1)} %get-tuple-element.33.x_ref.refs_0_, bf16[2,12288,2048]{2,1,0:T(8,128)(2,1)} %get-tuple-element.34.z_ref.refs_1_, ...), custom_call_target="tpu_custom_call" | custom-call | flops 118111600640 | bytes 150000000 | tf_op jit(solution)/shard_map/ffn_tiles/pallas_call | solution.py:125
  430.9 34.2 %token_sums.3.refs_2_ = f32[4096,2048]{1,0:T(8,128)} custom-call(s32[2,16]{1,0:T(2,128)} %get-tuple-element.83.lo_ref, s32[2,16]{1,0:T(2,128)} %get-tuple-element.82.hi_ref, s32[2,16,1,256]{3,2,1,0:T(1,128)} %add_select_fusion.2.pos_ref, bf16[2,4096,2048]{2,1,0:T(8,128)(2,1)} %get-tuple-element.35.refs_0_.refs_1_.refs_2_.refs_3_, ...), custom_call_target="tpu_custom_call" | custom-call | flops 20000000000 | bytes 100000000 | tf_op jit(solution)/shard_map/token_sums/pallas_call | solution.py:258
  468.7 0.7 add_select_fusion.1.pos_ref
  469.4 0.7 copy_select_fusion.1.pos_ref
  470.1 47.5 %pack_rows.4 = (bf16[2,12288,2048]{2,1,0:T(8,128)(2,1)}, bf16[2,12288,2048]{2,1,0:T(8,128)(2,1)}) custom-call(s32[2,16]{1,0:T(2,128)} %get-tuple-element.114.first_ref, s32[2,16]{1,0:T(2,128)} %get-tuple-element.113.window_ref, s32[2]{0:T(128)} %fusion.19.n_ref, ...), custom_call_target="tpu_custom_call", output_to_operand_aliasing={{0}: (7, {}), {1}: (8, {})} | custom-call | flops 30000001024 | bytes 200000000 | tf_op jit(solution)/shard_map/pack_rows/pallas_call | solution.py:76
  517.6 142.9 %ffn_tiles.4 = (bf16[2,12288,1408]{2,1,0:T(8,128)(2,1)}, bf16[2,12288,2816]{2,1,0:T(8,128)(2,1)}, bf16[2,4096,2048]{2,1,0:T(8,128)(2,1)}) custom-call(s32[2]{0:T(128)} %fusion.19.n_ref, bf16[2,12288,2048]{2,1,0:T(8,128)(2,1)} %get-tuple-element.36.x_ref.refs_0_, ...), custom_call_target="tpu_custom_call", output_to_operand_aliasing={{0}: (6, {}), {1}: (7, {})} | custom-call | flops 118111600640 | bytes 150000000 | tf_op jit(solution)/shard_map/ffn_tiles/pallas_call | solution.py:125
  660.5 34.8 %token_sums.4.refs_2_ = f32[4096,2048]{1,0:T(8,128)} custom-call(s32[2,16]{1,0:T(2,128)} %get-tuple-element.81.lo_ref, s32[2,16]{1,0:T(2,128)} %get-tuple-element.80.hi_ref, s32[2,16,1,256]{3,2,1,0:T(1,128)} %add_select_fusion.1.pos_ref, bf16[2,4096,2048]{2,1,0:T(8,128)(2,1)} %get-tuple-element.40.refs_0_.refs_1_.refs_2_.refs_3_, ...), custom_call_target="tpu_custom_call" | custom-call | flops 20000000000 | bytes 100000000 | tf_op jit(solution)/shard_map/token_sums/pallas_call | solution.py:258
  698.9 0.7 add_select_fusion.pos_ref
  699.6 0.7 copy_select_fusion.pos_ref
  700.3 43.8 %pack_rows.5 = (bf16[2,12288,2048]{2,1,0:T(8,128)(2,1)}, bf16[2,12288,2048]{2,1,0:T(8,128)(2,1)}) custom-call(s32[2,16]{1,0:T(2,128)} %get-tuple-element.116.first_ref, s32[2,16]{1,0:T(2,128)} %get-tuple-element.115.window_ref, s32[2]{0:T(128)} %fusion.18.n_ref, ...), custom_call_target="tpu_custom_call", output_to_operand_aliasing={{0}: (7, {}), {1}: (8, {})} | custom-call | flops 30000001024 | bytes 200000000 | tf_op jit(solution)/shard_map/pack_rows/pallas_call | solution.py:76
  744.1 142.7 %ffn_tiles.5 = (bf16[2,12288,1408]{2,1,0:T(8,128)(2,1)}, bf16[2,12288,2816]{2,1,0:T(8,128)(2,1)}, bf16[2,4096,2048]{2,1,0:T(8,128)(2,1)}) custom-call(s32[2]{0:T(128)} %fusion.18.n_ref, bf16[2,12288,2048]{2,1,0:T(8,128)(2,1)} %get-tuple-element.41.x_ref, ...), custom_call_target="tpu_custom_call", output_to_operand_aliasing={{0}: (6, {}), {1}: (7, {})} | custom-call | flops 118111600640 | bytes 150000000 | tf_op jit(solution)/shard_map/ffn_tiles/pallas_call | solution.py:125
  886.8 35.9 %token_sums.5 = f32[4096,2048]{1,0:T(8,128)} custom-call(s32[2,16]{1,0:T(2,128)} %get-tuple-element.85.lo_ref, s32[2,16]{1,0:T(2,128)} %get-tuple-element.84.hi_ref, s32[2,16,1,256]{3,2,1,0:T(1,128)} %add_select_fusion.pos_ref, bf16[2,4096,2048]{2,1,0:T(8,128)(2,1)} %get-tuple-element.45.refs_0_.refs_1_.refs_2_.refs_3_, ...), custom_call_target="tpu_custom_call" | custom-call | flops 20000000000 | bytes 100000000 | tf_op jit(solution)/shard_map/token_sums/pallas_call | solution.py:258
  924.4 84.6 %down_grads.3 = f32[2,1408,2048]{2,1,0:T(8,128)} custom-call(s32[2,16]{1,0:T(2,128)} %get-tuple-element.108.tile_ref, s32[2,16]{1,0:T(2,128)} %get-tuple-element.107.left_ref, bf16[2,12288,1408]{2,1,0:T(8,128)(2,1)} %get-tuple-element.50.h_ref, bf16[2,12288,2048]{2,1,0:T(8,128)(2,1)} %get-tuple-element.42.z_ref), custom_call_target="tpu_custom_call" | custom-call | flops 60000002048 | bytes 150000000 | tf_op jit(solution)/shard_map/down_grads/pallas_call | solution.py:208
  1009.0 171.1 %up_grads.3 = (f32[2,2048,1408]{2,1,0:T(8,128)}, f32[2,2048,1408]{2,1,0:T(8,128)}) custom-call(s32[2,16]{1,0:T(2,128)} %get-tuple-element.108.tile_ref, s32[2,16]{1,0:T(2,128)} %get-tuple-element.107.left_ref, bf16[2,12288,2048]{2,1,0:T(8,128)(2,1)} %get-tuple-element.41.x_ref, bf16[2,12288,2816]{2,1,0:T(8,128)(2,1)} %get-tuple-element.47.d_ref), custom_call_target="tpu_custom_call" | custom-call | flops 120000004096 | bytes 250000000 | tf_op jit(solution)/shard_map/up_grads/pallas_call | solution.py:178
  1180.1 11.7 fusion
  (147 shorter events, 22.3 us)
Async XLA Ops:
  7.2 252.6 %all-gather.9.cloned.1.call-start = ((), (), s32[]{:S(2)}) async-start(), calls=%async_computation.3 | async-start | bytes 18874368 | tf_op jit(solution)/shard_map/all_gather | solution.py:327
  13.1 9.6 copy-start.6
  13.1 9.6 copy-start.7
  13.1 9.6 copy-start.8
  13.1 246.7 %all-gather.11.cloned.1.call-start = ((), (), s32[]{:S(2)}) async-start(), calls=%async_computation.4 | async-start | bytes 18874368 | tf_op jit(solution)/shard_map/all_gather | solution.py:327
  19.0 451.1 %all-gather.13.cloned.1.call-start = ((), (), s32[]{:S(2)}) async-start(), calls=%async_computation.6 | async-start | bytes 18874368 | tf_op jit(solution)/shard_map/all_gather | solution.py:327
  19.7 450.3 %all-gather.15.cloned.1.call-start = ((), (), s32[]{:S(2)}) async-start(), calls=%async_computation.7 | async-start | bytes 18874368 | tf_op jit(solution)/shard_map/all_gather | solution.py:327
  20.3 680.0 %all-gather.17.cloned.1.call-start = ((), (), s32[]{:S(2)}) async-start(), calls=%async_computation.9 | async-start | bytes 18874368 | tf_op jit(solution)/shard_map/all_gather | solution.py:327
  20.9 679.4 %all-gather.19.cloned.1.call-start = ((), (), s32[]{:S(2)}) async-start(), calls=%async_computation.10 | async-start | bytes 18874368 | tf_op jit(solution)/shard_map/all_gather | solution.py:327
  21.5 1158.6 %reduce-scatter.4.cloned.1.call-start = ((), (), s32[]{:S(2)}) async-start(), calls=%async_computation.5 | async-start | bytes 37748736 | tf_op jit(solution)/shard_map/reduce_scatter | solution.py:338
  41.3 3.6 copy-start
  41.3 3.7 copy-start.2
  47.3 1.9 copy-start.11
  465.1 0.7 copy-start.3
  465.1 1.0 copy-start.5
  465.1 1.7 copy-start.12
  465.1 1.8 copy-start.20
  465.2 2.3 copy-start.17
  465.2 2.9 copy-start.14
  465.2 2.9 copy-start.16
  465.2 714.8 %reduce-scatter.6.cloned.1.call-start = ((), (), s32[]{:S(2)}) async-start(), calls=%async_computation.8 | async-start | bytes 37748736 | tf_op jit(solution)/shard_map/reduce_scatter | solution.py:338
  695.4 0.7 copy-start.1
  695.4 1.0 copy-start.4
  695.4 1.7 copy-start.10
  695.4 1.8 copy-start.22
  695.4 2.3 copy-start.18
  695.4 3.0 copy-start.13
  695.4 3.0 copy-start.15
  695.4 484.6 %reduce-scatter.8.cloned.1.call-start = ((), (), s32[]{:S(2)}) async-start(), calls=%async_computation.11 | async-start | bytes 37748736 | tf_op jit(solution)/shard_map/reduce_scatter | solution.py:338
  922.7 0.6 copy-start.23
  922.7 0.6 copy-start.21
  922.7 0.7 copy-start.19
  (1 other events, 0.5 us)
Sparse Core Ops, SparseCore 0:
  13.2 90.4 all-gather.8
  105.5 84.1 all-gather.10
  191.5 84.0 all-gather.12
  277.3 84.0 all-gather.14
  363.6 84.0 all-gather.16
  449.4 84.0 all-gather.18
  537.0 195.5 reduce-scatter.3
  736.1 196.2 reduce-scatter.5
  935.9 196.2 reduce-scatter.7
